TPU v7x, 256 devices: a whole 4x4x8 slice. The times are simulated.
256 devices in a mesh: ka: 8 (over y, x_lo), ga: 32 (over x_hi, z, core).
Axes of the slice: x: 4 (x_hi: 2, x_lo: 2; x = x_hi * 2 + x_lo), y: 4, z: 8, core: 2. Of those that a mesh axis runs over, the one named last changes fastest.
Arguments:
- coeffs: bfloat16 [8, 1, 65536, 2, 512], P('ka', None, 'ga'), may hold values from -0.5 to 0.5
- counts: int32 [8, 1], replicated, may hold values from 32768 to 65536
- block_map: int32 [8, 1, 2048], replicated, may hold values from 0 to 2047, as said below
- wrap: int32 [8, 1, 2048], replicated, may hold values from 0 to 31
Outputs:
- margins: float32 [8, 512, 1, 2, 512], P('ka', 'ga')
Inputs may be any that keep to these rules, and one draw needn't show every extreme that they name: For each k-point and line, block_map is a permutation of the 2048 blocks. Counting G-shards as runs of 64 blocks, at most 3 blocks of one shard have their partner blocks in any one shard, and for each k-point and line some pair of shards reaches 3.
All inputs are finite; a program needn't handle non-finite values.
Results may differ from a plain program's by a relative error of at most 0.0003.
Values may be sent and summed in bfloat16 or wider, within the bound.
A program may use at most 64 MiB of HBM per device.

v0:
```python
import jax
import jax.numpy as jnp
from jax import lax
from jax.sharding import PartitionSpec as P

BLK = 32


def from_behind(value, axis, steps):
    count = lax.axis_size(axis)
    pairs = [(source, (source + steps) % count) for source in range(count)]
    return lax.ppermute(value, axis, pairs)


def split_up(shard, dim, devices):
    before, after = (shard.shape[:dim], shard.shape[dim + 1 :])
    return jnp.moveaxis(shard.reshape(*before, devices, -1, *after), dim, 0)


def summed_on_arrival(shard, axis, dim):
    devices = lax.axis_size(axis)
    parts = lax.all_to_all(split_up(shard, dim, devices), axis, 0, 0, tiled=True)
    return jnp.sum(parts, axis=0)


def slot_table(dest, ranking, values, shard_count, capacity):
    shard_ids = jnp.arange(shard_count, dtype=jnp.int32)
    slot_ids = jnp.arange(capacity, dtype=jnp.int32)
    hit = (dest[:, :, None, None] == shard_ids[None, None, :, None]) & (
        ranking[:, :, None, None] == slot_ids[None, None, None, :]
    )
    return jnp.sum(jnp.where(hit, values[:, :, None, None], 0), axis=1)


def pick_rows(source, picks):
    return jax.vmap(lambda rows_in, index_in: jnp.take(rows_in, index_in, axis=0))(source, picks)


def local(coeffs, counts, block_map, wrap):
    held_k = coeffs[0]
    line_count, g_rows, _, band_count = held_k.shape
    shard_count = lax.axis_size("ga")
    per_shard = g_rows // BLK
    block_total = block_map.shape[-1]
    capacity = block_total // (shard_count * shard_count) + 1
    k_index = lax.axis_index("ka")
    g_index = lax.axis_index("ga")
    k_total = counts.shape[0]
    count_here = counts[k_index]
    count_next = counts[(k_index + 1) % k_total]
    block_src = block_map[k_index]
    wrap_src = wrap[k_index]
    lane_ids = jnp.arange(BLK, dtype=jnp.int32)
    block_mine = lax.dynamic_slice_in_dim(block_src, g_index * per_shard, per_shard, 1)
    wrap_mine = lax.dynamic_slice_in_dim(wrap_src, g_index * per_shard, per_shard, 1)
    lane_shift = (lane_ids[None, None, :] + wrap_mine[:, :, None]) % BLK
    src_rows = block_mine[:, :, None] * BLK + lane_shift
    own_rows = g_index * g_rows + jnp.arange(g_rows, dtype=jnp.int32).reshape(per_shard, BLK)
    usable = (own_rows[None] < count_here[:, None, None]) & (src_rows < count_next[:, None, None])
    usable = usable.reshape(line_count, g_rows)
    masked_k = jnp.where(usable[:, :, None, None], held_k, jnp.zeros((), held_k.dtype))
    source_dev = block_mine // per_shard
    same_dev = source_dev[:, :, None] == source_dev[:, None, :]
    earlier = jnp.arange(per_shard)[:, None] > jnp.arange(per_shard)[None, :]
    rank_mine = jnp.sum((same_dev & earlier[None]).astype(jnp.int32), axis=2)
    coming = from_behind(held_k, "ka", -1)
    blocks_held = masked_k.reshape(line_count, per_shard, BLK, 2, band_count)
    back_lanes = (lane_ids[None, None, :] - wrap_mine[:, :, None]) % BLK
    rotated = jax.vmap(jax.vmap(lambda rows_in, index_in: jnp.take(rows_in, index_in, axis=0)))(
        blocks_held, back_lanes
    )
    local_ids = jnp.arange(per_shard, dtype=jnp.int32)[None, :]
    send_table = slot_table(source_dev, rank_mine, local_ids, shard_count, capacity)
    outgoing = pick_rows(rotated, send_table.reshape(line_count, -1))
    outgoing = outgoing.reshape(line_count, shard_count, capacity * BLK, 2, band_count)
    incoming = lax.all_to_all(outgoing, "ga", split_axis=1, concat_axis=1, tiled=True)
    incoming = incoming.reshape(line_count, shard_count * capacity * BLK, 2, band_count)
    inverse = jax.vmap(
        lambda perm_in: jnp.zeros((block_total,), jnp.int32)
        .at[perm_in]
        .set(jnp.arange(block_total, dtype=jnp.int32))
    )(block_src)
    target_mine = lax.dynamic_slice_in_dim(inverse, g_index * per_shard, per_shard, 1)
    sender = target_mine // per_shard
    to_me = block_src // per_shard == g_index
    rank_to_me = (
        jnp.cumsum(to_me.reshape(line_count, shard_count, per_shard).astype(jnp.int32), axis=2) - 1
    ).reshape(line_count, block_total)
    rank_sent = jnp.take_along_axis(rank_to_me, target_mine, axis=1)
    row_index = (
        (sender * capacity + rank_sent)[:, :, None] * BLK + lane_ids[None, None, :]
    ).reshape(line_count, g_rows)
    left_side = pick_rows(incoming, row_index)
    products = jnp.einsum("lgcm,lgdn->mlcdn", left_side, coming, preferred_element_type=jnp.float32)
    real_part = products[:, :, 0, 0] + products[:, :, 1, 1]
    imag_part = products[:, :, 0, 1] - products[:, :, 1, 0]
    result = summed_on_arrival(jnp.stack([real_part, imag_part], axis=2), "ga", 0)
    return result[None]


def solution(mesh):
    placed = (P("ka", None, "ga", None, None), P(), P(), P())
    return jax.shard_map(
        local,
        mesh=mesh,
        in_specs=placed,
        out_specs=P("ka", "ga", None, None, None),
        check_vma=False,
    )
```

profile of v0, /device:TPU:10, one launch (start us, length us, event | category | flops | bytes accessed | tf_op | source)
XLA Modules:
  0.0 326.2 jit_solution(14142816753360796618)
XLA Ops:
  0.0 0.8 and_select_fusion.1
  0.8 0.2 convert_reduce_fusion
  1.0 0.2 select_reduce_fusion
  1.2 0.1 copy.15
  1.3 0.1 fusion.40
  1.4 0.1 compare_select_fusion
  1.5 0.1 reshape.1008
  1.6 0.1 reshape.984
  1.7 0.1 copy.14
  1.9 0.1 broadcast_in_dim.90
  2.0 0.1 broadcast_in_dim.91
  2.1 1.4 constant_dynamic-slice_fusion.1
  3.5 1.4 compare_and_fusion
  4.9 6.8 %broadcast_select_fusion.2 = bf16[1,64,32,2,512]{4,3,2,1,0:T(2,128)(2,1)} fusion(bf16[1,64,32,2,512]{4,3,2,1,0:T(2,128)(2,1)} %bitcast.93, pred[64,32]{1,0:T(8,128)(4,1)S(1)} %get-tuple-element.10), kind=kLoop, calls=%fused_computation.7 | loop fusion | flops 2097152 | bytes 8390656 | tf_op jit(solution)/shard_map/jit(_where)/select_n | solution.py:61
  11.7 25.9 %gather_fusion.1 = bf16[2048,2,512]{2,1,0:T(2,128)(2,1)} fusion(bf16[1,64,32,2,512]{4,3,2,1,0:T(2,128)(2,1)} %broadcast_select_fusion.2, s32[2048]{0:T(1024)S(1)} %reshape.1008), kind=kCustom, calls=%fused_computation.1 | custom fusion | bytes 8413184 | tf_op jit(solution)/shard_map/vmap(vmap(jit(_take)))/gather | solution.py:69
  37.6 6.8 %broadcast_select_fusion.3 = bf16[1,64,32,2,512]{4,3,2,1,0:T(2,128)(2,1)} fusion(bf16[1,64,32,2,512]{4,3,2,1,0:T(2,128)(2,1)} %bitcast.94, pred[64,32]{1,0:T(8,128)(4,1)S(1)} %get-tuple-element.9), kind=kLoop, calls=%fused_computation.8 | loop fusion | flops 2097152 | bytes 8390656 | tf_op jit(solution)/shard_map/vmap(vmap(jit(_take)))/select_n | solution.py:69
  44.4 17.5 %gather_fusion.2 = bf16[96,32,2,512]{3,2,1,0:T(2,128)(2,1)} fusion(bf16[1,64,32,2,512]{4,3,2,1,0:T(2,128)(2,1)} %broadcast_select_fusion.3, s32[96]{0:T(128)S(1)} %or_bitcast_fusion), kind=kCustom, calls=%fused_computation.2 | custom fusion | bytes 12583680 | tf_op jit(solution)/shard_map/vmap(jit(_take))/gather | solution.py:36
  61.9 10.5 %broadcast_select_fusion = bf16[1,32,96,2,512]{4,3,2,0,1:T(2,128)(2,1)} fusion(bf16[1,32,96,2,512]{4,3,2,0,1:T(2,128)(2,1)} %bitcast.92, pred[32,96]{1,0:T(8,128)(4,1)S(1)} %broadcast_in_dim.91), kind=kLoop, calls=%fused_computation.5 | loop fusion | flops 3145728 | bytes 12585984 | tf_op jit(solution)/shard_map/vmap(jit(_take))/select_n | solution.py:36
  72.5 10.5 %all-to-all-start = ((bf16[1,32,96,2,512]{4,3,2,0,1:T(2,128)(2,1)}), bf16[1,32,96,2,512]{4,3,2,0,1:T(2,128)(2,1)}, u32[]{:S(2)}, u32[]{:S(2)}) async-start(bf16[1,32,96,2,512]{4,3,2,0,1:T(2,128)(2,1)} %broadcast_select_fusion), calls=%async_computation | async-start | bytes 12582912 | tf_op jit(solution)/shard_map/all_to_all | solution.py:76
  83.0 0.0 copy-start.1
  83.0 0.0 copy-start.2
  83.0 4.8 %copy.31 = bf16[1,1,2048,2,512]{4,2,3,1,0:T(8,128)(2,1)} copy(bf16[1,1,2048,2,512]{4,3,2,1,0:T(2,128)(2,1)} %param.4) | data formatting | bytes 8388608 | tf_op args[0]
  87.9 1.4 collective-permute-start
  89.3 0.7 dynamic-slice_reduce_fusion
  90.0 0.1 squeeze.16
  90.1 0.2 reduce_window_sum.11
  90.3 0.1 reshape.996
  90.4 0.7 compare_select_fusion.3
  91.1 0.1 fusion.30
  91.3 0.1 and_reduce_fusion
  91.4 8.2 %scatter_custom_fusion = s32[2048]{0:T(1024)S(1)} fusion(s32[2048]{0:T(1024)S(1)} %broadcast_select_fusion.4, s32[2048]{0:T(1024)S(1)} %iota.74, s32[]{:T(128)} %constant.157.clone.1), kind=kCustom, calls=%fused_computation.86 | custom fusion | bytes 8196
  99.6 0.1 fusion.43
  99.7 0.8 gather_fusion
  100.5 0.1 multiply_bitcast_fusion
  100.6 0.1 add.345
  100.6 0.1 add.371
  100.7 0.1 add.346
  100.8 0.1 add.373
  100.9 0.1 add.348
  101.1 124.3 %all-to-all-done = bf16[1,32,96,2,512]{4,3,2,0,1:T(2,128)(2,1)} async-done(((bf16[1,32,96,2,512]{4,3,2,0,1:T(2,128)(2,1)}), bf16[1,32,96,2,512]{4,3,2,0,1:T(2,128)(2,1)}, u32[]{:S(2)}, u32[]{:S(2)}) %all-to-all-start) | async-done | bytes 6291488 | tf_op jit(solution)/shard_map/all_to_all | solution.py:76
  225.4 24.6 %gather_fusion.3 = bf16[2048,2,512]{2,1,0:T(2,128)(2,1)} fusion(bf16[1,3072,2,512]{3,2,1,0:T(2,128)(2,1)} %bitcast.16, s32[2048]{0:T(1024)S(1)} %bitcast.91), kind=kCustom, calls=%fused_computation.3 | custom fusion | bytes 8404992 | tf_op jit(solution)/shard_map/vmap(jit(_take))/gather | solution.py:36
  250.0 8.7 %fusion.3 = bf16[2048,2,512,1]{2,1,0,3:T(2,128)(2,1)S(1)} fusion(bf16[2048,2,512]{2,1,0:T(2,128)(2,1)} %gather_fusion.3, pred[2048]{0:T(1024)(128)(4,1)S(1)} %compare_and_fusion.1), kind=kLoop, calls=%fused_computation.13 | loop fusion | flops 2097152 | bytes 8390656 | tf_op jit(solution)/shard_map/vmap(jit(_take))/select_n | solution.py:36
  258.7 6.5 %fusion.4 = f32[512,1,2,2,512]{4,0,3,2,1:T(8,128)S(1)} fusion(bf16[1,2048,2,512]{3,1,2,0:T(8,128)(2,1)} %collective-permute-done, bf16[2048,2,512,1]{2,1,0,3:T(2,128)(2,1)S(1)} %fusion.3), kind=kOutput, calls=%fused_computation.14 | convolution fusion | flops 4294967296 | bytes 12582912 | tf_op jit(solution)/shard_map/lgcm,lgdn->mlcdn/dot_general | solution.py:94
  265.2 0.5 slice_add_fusion
  265.7 0.2 pad_maximum_fusion
  265.9 59.5 %all_to_all.10 = f32[32,16,1,2,512]{4,1,3,2,0:T(8,128)S(1)} all-to-all(f32[32,16,1,2,512]{4,1,3,2,0:T(8,128)S(1)} %pad_maximum_fusion), channel_id=1, replica_groups=mesh['ka'=8,'ga'=32] {'ga'}, dimensions={0} | all-to-all | bytes 4194304 | tf_op jit(solution)/shard_map/all_to_all | solution.py:22
  325.4 0.1 reduce_sum.29
  325.5 0.7 copy.21
  (28 shorter events, 0.2 us)
Async XLA Ops:
  0.0 1.3 copy-start
  72.5 152.9 %all-to-all-start = ((bf16[1,32,96,2,512]{4,3,2,0,1:T(2,128)(2,1)}), bf16[1,32,96,2,512]{4,3,2,0,1:T(2,128)(2,1)}, u32[]{:S(2)}, u32[]{:S(2)}) async-start(bf16[1,32,96,2,512]{4,3,2,0,1:T(2,128)(2,1)} %broadcast_select_fusion), calls=%async_computation | async-start | bytes 12582912 | tf_op jit(solution)/shard_map/all_to_all | solution.py:76
  83.0 8.1 %copy-start.1 = (s32[2]{0:T(128)S(1)}, s32[2]{0:T(128)}, u32[]{:S(2)}) copy-start(s32[2]{0:T(128)} %constant.181) | copy-start | bytes 28
  83.0 8.2 %copy-start.2 = (s32[2]{0:T(128)S(1)}, s32[2]{0:T(128)}, u32[]{:S(2)}) copy-start(s32[2]{0:T(128)} %constant.184) | copy-start | bytes 28
  87.9 170.8 %collective-permute-start = (bf16[1,2048,2,512]{3,1,2,0:T(8,128)(2,1)}, bf16[1,2048,2,512]{3,1,2,0:T(8,128)(2,1)}, u32[]{:S(2)}, u32[]{:S(2)}) collective-permute-start(bf16[1,2048,2,512]{3,1,2,0:T(8,128)(2,1)} %bitcast.90), channel_id=1, source_target_pairs={{0,224},{32,0},{64,32},{96,64},{128,96},{160,128},{192,160},{224,1... | collective-permute-start | bytes 12582920 | tf_op jit(solution)/shard_map/ppermute | solution.py:12
where the time goes:
time: 328 us; the launch traced here: 326 us
  waiting for transfers between devices  124 us (38%)
  local copies, waits for them, and re-layouts  85.9 us (26%)
  blocking collectives  59.5 us (18%)
  other arithmetic  37.8 us (12%)
  starting transfers between devices  12 us (4%)
  matrix products  6.45 us (2%)
    all_to_all x1, waiting for transfers between devices, local(): lax.all_to_all(outgoing, 'ga', split_axis=1, concat_axis=1, tiled=True)  124 us
    all_to_all x1, blocking collectives, summed_on_arrival(): lax.all_to_all(split_up(shard, dim, devices), axis, 0, 0, tiled=True)  59.5 us
    gather x4, local copies, waits for them, and re-layouts, pick_rows(): jnp.take(rows_in, index_in, axis=0)  42.1 us
    gather x2, local copies, waits for them, and re-layouts, local(): jnp.take(rows_in, index_in, axis=0)  26 us
    select_n x4, other arithmetic, pick_rows(): jnp.take(rows_in, index_in, axis=0)  19.3 us
    unnamed x10, local copies, waits for them, and re-layouts  13.1 us
    all_to_all x1, starting transfers between devices, local(): lax.all_to_all(outgoing, 'ga', split_axis=1, concat_axis=1, tiled=True)  10.5 us
    select_n x2, other arithmetic, local(): jnp.take(rows_in, index_in, axis=0)  6.9 us
  transfers between devices with their start and end apart: 2, of which 1 were waited for; matrix products, arithmetic and copies ran while one was open for 15% of the time, Pallas kernels for 0%

commit v1 on v0

v1 whole, which is shorter than its diff:
```python
import functools

import jax
import jax.numpy as jnp
from jax import lax
from jax.experimental import pallas as pl
from jax.experimental.pallas import tpu as pltpu
from jax.sharding import PartitionSpec as P

MESH = pl.DeviceIdType.MESH
BLK = 32
ROWS = 2 * BLK
CAP = 3
NS = 32
NZ = 8
LANE = 128
NQ = 4
GRP = 4
NG = NS // GRP
STEP = CAP * ROWS
AHEAD = 4


def rem(a, b):
    return lax.rem(a, jnp.int32(b))


def div(a, b):
    return lax.div(a, jnp.int32(b))


def offset(grp, u):
    d = div(grp + 1, 2)
    edge = 1 - div(rem(grp, 7) + 6, 7)
    odd = u % 2
    dz = d * (1 - 2 * odd * (1 - edge))
    dx = ((u + 1) // 2) % 2
    dc = edge * odd + (1 - edge) * rem(grp + 1, 2)
    return dz, dx, dc


def shifted(x, z, c, off, sign):
    dz, dx, dc = off
    return rem(x + dx, 2) * 16 + rem(z + sign * dz + 16, NZ) * 2 + rem(c + dc, 2)


def kernel(send_tab, recv_tab, cin, out, send, recv, left, acc, rs1, rs2, rs3,
           ssem, rsem, s1sem, r1sem, s2sem, r2sem, s3sem, r3sem):
    k = lax.axis_index("ka")
    g = lax.axis_index("ga")
    x, z, c = div(g, 16), rem(div(g, 2), NZ), rem(g, 2)
    k_to, k_from = rem(k + 7, 8), rem(k + 1, 8)
    core_peer = x * 16 + z * 2 + (1 - c)
    x_peer = (1 - x) * 16 + z * 2 + c

    def z_peer(dz):
        return x * 16 + rem(z + dz, NZ) * 2 + c

    barrier = pltpu.get_barrier_semaphore()

    def greet(s, carry):
        pl.semaphore_signal(barrier, inc=1, device_id=(k_from, s), device_id_type=MESH)
        return carry

    lax.fori_loop(0, NS, greet, 0)
    for peer in [core_peer, x_peer] + [z_peer(dz) for dz in range(1, NZ)]:
        pl.semaphore_signal(barrier, inc=1, device_id=(k, peer), device_id_type=MESH)

    def stage(it):
        q, grp = div(it, NG), rem(it, NG)
        for u in range(GRP):
            t = shifted(x, z, c, offset(grp, u), 1)
            for r in range(CAP):
                send[q, grp * GRP + u, r * ROWS:(r + 1) * ROWS, :] = cin[q, send_tab[t * CAP + r]]

    def exchange(it, u):
        q, grp = div(it, NG), rem(it, NG)
        j = grp * GRP + u
        t = shifted(x, z, c, offset(grp, u), 1)
        return pltpu.make_async_remote_copy(
            src_ref=send.at[q, j], dst_ref=recv.at[q, j], send_sem=ssem.at[q, j], recv_sem=rsem.at[q, j],
            device_id=(k_to, t), device_id_type=MESH)

    def launch(it):
        for u in range(GRP):
            exchange(it, u).start()

    row = lax.broadcasted_iota(jnp.int32, (2 * ROWS, 4 * ROWS), 0)
    col = lax.broadcasted_iota(jnp.int32, (2 * ROWS, 4 * ROWS), 1)
    left_lane = rem(div(row, 2), BLK)
    right_lane = rem(div(col, 2), BLK)
    first = row < ROWS
    same_slot = div(row, ROWS) == rem(div(col, ROWS), 2)
    straight = col < 2 * ROWS
    same_part = rem(row, 2) == rem(col, 2)
    sign = jnp.where(straight, jnp.where(same_part, 1.0, 0.0),
                     jnp.where(same_part, 0.0, jnp.where(rem(row, 2) == 0, 1.0, -1.0)))
    pattern = jnp.where(same_slot, sign, 0.0)

    def build(grp):
        for pair in range(GRP * CAP // 2):
            slots = []
            for h in range(2):
                u, r = divmod(2 * pair + h, CAP)
                s = shifted(x, z, c, offset(grp, u), -1)
                slots.append([recv_tab[n * NS * CAP + s * CAP + r] for n in range(4)])
            (b0, w0, l0, r0), (b1, w1, l1, r1) = slots
            w = jnp.where(first, w0, w1)
            hit = left_lane == ((right_lane - w) & (BLK - 1))
            hit = hit & (left_lane < jnp.where(first, l0, l1)) & (right_lane < jnp.where(first, r0, r1))
            pick = jnp.where(hit, pattern, 0.0).astype(jnp.bfloat16)
            cols = pl.ds(pl.multiple_of(grp * (GRP * STEP) + pair * 2 * ROWS, LANE), 2 * ROWS)
            for q in range(NQ):
                held = jnp.concatenate([cin[q, b0], cin[q, b1]], axis=0)
                moved = lax.dot_general(held, pick, (((0,), (0,)), ((), ())),
                                        preferred_element_type=jnp.float32).astype(jnp.bfloat16)
                for ii in range(8):
                    i = q * 8 + ii
                    ix, iz, ic = i // 16, (i // 2) % NZ, i % 2
                    base = ((ic * 2 + ix) * NZ + iz) * 32
                    part = moved[ii * 16:(ii + 1) * 16]
                    left[base:base + 16, cols] = part[:, :LANE]
                    left[base + 16:base + 32, cols] = part[:, LANE:]

    def multiply(it):
        q, grp = div(it, NG), rem(it, NG)
        for u in range(GRP):
            exchange(it, u).wait_recv()
        j0 = grp * GRP
        cols = pl.ds(pl.multiple_of(grp * (GRP * STEP), LANE), GRP * STEP)
        right = recv[q, pl.ds(j0, GRP)].reshape(GRP * STEP, LANE)
        part = 256

        def strip(n, carry):
            rows = pl.ds(pl.multiple_of(n * part, part), part)
            val = jnp.dot(left[rows, cols], right, preferred_element_type=jnp.float32)

            @pl.when(grp == 0)
            def _():
                acc[q, rows] = val

            @pl.when(grp > 0)
            def _():
                acc[q, rows] += val

            return carry

        lax.fori_loop(0, 1024 // part, strip, 0)

    def half(which):
        return pl.ds(pl.multiple_of(which * 512, 512), 512)

    def quarter(cc, xx):
        return pl.ds(pl.multiple_of(cc * 512 + xx * 256, 256), 256)

    def piece(cc, xx, zz):
        return pl.ds(pl.multiple_of(cc * 512 + xx * 256 + zz * 32, 32), 32)

    def to_core(q):
        return pltpu.make_async_remote_copy(
            src_ref=acc.at[q, half(1 - c)], dst_ref=rs1.at[q], send_sem=s1sem.at[q], recv_sem=r1sem.at[q],
            device_id=(k, core_peer), device_id_type=MESH)

    def to_x(q):
        return pltpu.make_async_remote_copy(
            src_ref=acc.at[q, quarter(c, 1 - x)], dst_ref=rs2.at[q], send_sem=s2sem.at[q], recv_sem=r2sem.at[q],
            device_id=(k, x_peer), device_id_type=MESH)

    def to_z(q, dz):
        return pltpu.make_async_remote_copy(
            src_ref=acc.at[q, piece(c, x, rem(z + dz, NZ))], dst_ref=rs3.at[q, dz],
            send_sem=s3sem.at[q, dz], recv_sem=r3sem.at[q, dz],
            device_id=(k, z_peer(dz)), device_id_type=MESH)

    def after_core(q):
        to_core(q).wait_recv()
        acc[q, half(c)] += rs1[q]
        to_x(q).start()

    def after_x(q):
        to_x(q).wait_recv()
        acc[q, quarter(c, x)] += rs2[q]
        for dz in range(1, NZ):
            to_z(q, dz).start()

    def finish(q):
        total = acc[q, piece(c, x, z)]
        for dz in range(1, NZ):
            to_z(q, dz).wait_recv()
            total = total + rs3[q, dz]
        out[0, :, q * LANE:(q + 1) * LANE] = total[:16]
        out[1, :, q * LANE:(q + 1) * LANE] = total[16:]

    stage(jnp.int32(0))
    pl.semaphore_wait(barrier, NS + 2 + NZ - 1)

    def start(it, carry):
        launch(it)
        stage(it + 1)
        return carry

    lax.fori_loop(0, AHEAD, start, 0)
    total_its = NQ * NG

    def body(it, carry):
        q, grp = div(it, NG), rem(it, NG)

        @pl.when(it + AHEAD < total_its)
        def _():
            launch(it + AHEAD)

        @pl.when(it + AHEAD + 1 < total_its)
        def _():
            stage(it + AHEAD + 1)

        @pl.when(q == 0)
        def _():
            build(grp)

        @pl.when((q > 0) & (grp == 0))
        def _():
            to_core(q - 1).start()

        @pl.when((q > 0) & (grp == 2))
        def _():
            after_core(q - 1)

        @pl.when((q > 0) & (grp == 4))
        def _():
            after_x(q - 1)

        multiply(it)
        return carry

    lax.fori_loop(0, total_its, body, 0)
    last = NQ - 1
    to_core(last).start()
    after_core(last)
    after_x(last)
    for q in range(NQ):
        finish(q)

    def drain(it, carry):
        for u in range(GRP):
            exchange(it, u).wait_send()
        return carry

    lax.fori_loop(0, total_its, drain, 0)
    for q in range(NQ):
        to_core(q).wait_send()
        to_x(q).wait_send()
        for dz in range(1, NZ):
            to_z(q, dz).wait_send()


def slots(hit, values):
    depth = hit.shape[-1]
    tri = (jnp.arange(depth)[:, None] <= jnp.arange(depth)[None, :]).astype(jnp.bfloat16)
    place = jnp.dot(hit.astype(jnp.bfloat16), tri, preferred_element_type=jnp.float32).astype(jnp.int32) - 1
    chosen = hit[:, None, :] & (place[:, None, :] == jnp.arange(CAP)[None, :, None])
    return [jnp.sum(jnp.where(chosen, v, 0), axis=-1).reshape(-1) for v in values]


def local(coeffs, counts, block_map, wrap):
    k = lax.axis_index("ka")
    g = lax.axis_index("ga")
    per = block_map.shape[-1] // NS
    shard = jnp.arange(NS, dtype=jnp.int32)
    to_map = block_map[(k + 7) % 8, 0].reshape(NS, per)
    (send_tab,) = slots(to_map // per == g, [to_map[:, None, :] % per])
    mine = lax.dynamic_slice_in_dim(block_map[k, 0], g * per, per)
    turn = lax.dynamic_slice_in_dim(wrap[k, 0], g * per, per)
    ids = jnp.arange(per, dtype=jnp.int32)
    left_lim = counts[k, 0] - (g * per + ids) * BLK
    right_lim = counts[(k + 1) % 8, 0] - mine * BLK
    recv_tab = jnp.concatenate(slots(mine[None, :] // per == shard[:, None], [ids, turn, left_lim, right_lim]))
    cin = coeffs.reshape(per, BLK, 2, NQ, LANE).transpose(3, 0, 1, 2, 4).reshape(NQ, per, ROWS, LANE)
    vmem = pl.BlockSpec(memory_space=pltpu.VMEM)
    smem = pl.BlockSpec(memory_space=pltpu.SMEM)
    dma = pltpu.SemaphoreType.DMA
    out = pl.pallas_call(
        kernel,
        out_shape=jax.ShapeDtypeStruct((2, 16, NQ * LANE), jnp.float32),
        in_specs=[smem, smem, vmem],
        out_specs=vmem,
        scratch_shapes=[
            pltpu.VMEM((NQ, NS, STEP, LANE), jnp.bfloat16),
            pltpu.VMEM((NQ, NS, STEP, LANE), jnp.bfloat16),
            pltpu.VMEM((1024, NS * STEP), jnp.bfloat16),
            pltpu.VMEM((NQ, 1024, LANE), jnp.float32),
            pltpu.VMEM((NQ, 512, LANE), jnp.float32),
            pltpu.VMEM((NQ, 256, LANE), jnp.float32),
            pltpu.VMEM((NQ, NZ, 32, LANE), jnp.float32),
            dma((NQ, NS)), dma((NQ, NS)), dma((NQ,)), dma((NQ,)), dma((NQ,)), dma((NQ,)),
            dma((NQ, NZ)), dma((NQ, NZ)),
        ],
        compiler_params=pltpu.CompilerParams(
            collective_id=0, has_side_effects=True, vmem_limit_bytes=48 << 20),
    )(send_tab, recv_tab, cin)
    return out.transpose(1, 0, 2)[None, :, None]


def solution(mesh):
    placed = (P("ka", None, "ga", None, None), P(), P(), P())
    return jax.shard_map(
        local,
        mesh=mesh,
        in_specs=placed,
        out_specs=P("ka", "ga", None, None, None),
        check_vma=False,
    )
```

time: 328 us -> 230 us (0.70)
  Pallas kernels: 0 us -> 200 us
  waiting for transfers between devices: 124 us -> 0 us
  local copies, waits for them, and re-layouts: 85.9 us -> 22.7 us
  blocking collectives: 59.5 us -> 0 us
  other arithmetic: 37.8 us -> 2.67 us
  starting transfers between devices: 12 us -> 0 us
  matrix products: 6.45 us -> 0.26 us
    pallas_call x0 -> x1, Pallas kernels: none -> 200 us  [local(): pl.pallas_call(kernel, out_shape=jax.ShapeDtypeStruct((2, 16, NQ * LANE),...]
    all_to_all x1 -> x0, waiting for transfers between devices: 124 us -> none  [local(): lax.all_to_all(outgoing, 'ga', split_axis=1, concat_axis=1, tiled=True)]
    gather x7 -> x0, local copies, waits for them, and re-layouts: 68.9 us -> none  [the longest x4 42.1 us: pick_rows(): jnp.take(rows_in, index_in, axis=0)]
    all_to_all x1 -> x0, blocking collectives: 59.5 us -> none  [summed_on_arrival(): lax.all_to_all(split_up(shard, dim, devices), axis, 0, 0, tiled=True)]
    select_n x9 -> x1, other arithmetic: 34.5 us -> 0.01 us  [local(): send_tab, = slots(to_map // per == g, [to_map[:, None, :] % per])]
    reshape x1 -> x7, local copies, waits for them, and re-layouts: 0.1 us -> 17.1 us  [the longest x2 16.6 us: local(): coeffs.reshape(per, BLK, 2, NQ, LANE).transpose(3, 0, 1, 2, 4)]
    unnamed x10 -> x4, local copies, waits for them, and re-layouts: 13.1 us -> 2.19 us
    all_to_all x1 -> x0, starting transfers between devices: 10.5 us -> none  [local(): lax.all_to_all(outgoing, 'ga', split_axis=1, concat_axis=1, tiled=True)]
  transfers between devices with their start and end apart: 2 -> 0, of which waited for: 1 -> 0; matrix products, arithmetic and copies ran while one was open for 15% -> 0% of each run, Pallas kernels for 0% -> 0%
where the time goes in v1:
time: 230 us; the launch traced here: 226 us
  Pallas kernels  200 us (87%)
  local copies, waits for them, and re-layouts  22.7 us (10%)
  other arithmetic  2.67 us (1%)
    pallas_call x1, Pallas kernels, local(): pl.pallas_call(kernel, out_shape=jax.ShapeDtypeStruct((2, 16, NQ * LANE),...  200 us
    reshape x2, local copies, waits for them, and re-layouts, local(): coeffs.reshape(per, BLK, 2, NQ, LANE).transpose(3, 0, 1, 2, 4)  16.6 us

profile of v1, /device:TPU:10, one launch (start us, length us, event | category | flops | bytes accessed | tf_op | source)
XLA Modules:
  0.0 225.7 jit_solution(6764888559540327882)
XLA Ops:
  0.0 0.0 copy-start
  0.0 1.4 constant_dynamic-slice_fusion.1
  1.4 2.1 multiply_subtract_fusion
  3.5 0.0 copy-done
  3.5 0.1 fusion.8
  3.6 0.7 dynamic-slice_reduce_fusion
  4.3 0.1 reshape_squeeze.3
  4.4 0.1 fusion
  4.5 0.3 select_reduce_fusion.3
  4.8 0.1 copy.10
  4.9 0.1 reshape.160
  5.0 0.1 copy.13
  5.1 0.1 reshape.163
  5.2 0.1 copy.12
  5.3 0.1 reshape.162
  5.4 0.1 copy.11
  5.5 0.1 reshape.161
  5.6 0.1 pad_add_fusion.recv_tab
  5.7 0.1 fusion.1
  5.8 0.2 select_reduce_fusion.4
  6.0 0.1 copy.9
  6.1 0.1 reshape.159.send_tab
  6.2 7.6 %reshape.164 = bf16[64,32,2,4,128]{4,3,2,1,0:T(4,128)(2,1)} reshape(bf16[1,1,2048,2,512]{4,3,2,1,0:T(2,128)(2,1)} %param.4) | data formatting | bytes 8388608 | tf_op jit(solution)/shard_map/reshape | solution.py:277
  13.8 9.0 %copy.14 = bf16[64,32,2,4,128]{4,2,1,0,3:T(2,128)(2,1)} copy(bf16[64,32,2,4,128]{4,3,2,1,0:T(4,128)(2,1)} %reshape.164) | data formatting | bytes 8388608 | tf_op jit(solution)/shard_map/reshape | solution.py:277
  22.8 0.0 copy-start.1
  22.8 2.2 copy-done.1
  25.0 200.0 %shard_map.46 = f32[2,16,512]{2,1,0:T(8,128)S(1)} custom-call(s32[96]{0:T(128)S(1)} %reshape.159.send_tab, s32[384]{0:T(512)S(1)} %pad_add_fusion.recv_tab, bf16[4,64,64,128]{3,2,1,0:T(8,128)(2,1)S(1)} %bitcast.17), custom_call_target="tpu_custom_call" | custom-call | tf_op jit(solution)/shard_map/pallas_call | solution.py:281
  225.0 0.7 copy.15
  (3 shorter events, 0.0 us)
Async XLA Ops:
  0.0 3.5 %copy-start = (s32[8,1,2048]{2,1,0:T(1,128)S(1)}, s32[8,1,2048]{2,1,0:T(1,128)}, u32[]{:S(2)}) copy-start(s32[8,1,2048]{2,1,0:T(1,128)} %param.7) | copy-start | bytes 196612
  22.8 2.2 copy-start.1

commit v2 on v1

--- a/solution.py
+++ b/solution.py
@@ -19,6 +19,9 @@
 NG = NS // GRP
 STEP = CAP * ROWS
 AHEAD = 4
+RELAYED = (1, 2)
+DIRECT = (0, 3)
+NR = len(RELAYED)
 
 
 def rem(a, b):
@@ -30,6 +33,7 @@
 
 
 def offset(grp, u):
+    grp = NG - 1 - grp
     d = div(grp + 1, 2)
     edge = 1 - div(rem(grp, 7) + 6, 7)
     odd = u % 2
@@ -44,8 +48,52 @@
     return rem(x + dx, 2) * 16 + rem(z + sign * dz + 16, NZ) * 2 + rem(c + dc, 2)
 
 
-def kernel(send_tab, recv_tab, cin, out, send, recv, left, acc, rs1, rs2, rs3,
-           ssem, rsem, s1sem, r1sem, s2sem, r2sem, s3sem, r3sem):
+def prepare(counts, block_map, wrap, coeffs, cin, send_tab, recv_tab, sem):
+    copies = [pltpu.make_async_copy(coeffs.at[:, :, pl.ds(q * LANE, LANE)], cin.at[q], sem.at[q]) for q in range(NQ)]
+    for copy in copies:
+        copy.start()
+    k = lax.axis_index("ka")
+    g = lax.axis_index("ga")
+    k_to, k_from = rem(k + 7, 8), rem(k + 1, 8)
+
+    def shape_iota(rows, dim):
+        return lax.broadcasted_iota(jnp.int32, (rows, LANE), dim)
+
+    tri = (shape_iota(LANE, 0) <= shape_iota(LANE, 1)) & (div(shape_iota(LANE, 0), 64) == div(shape_iota(LANE, 1), 64))
+    tri = jnp.where(tri, 1.0, 0.0).astype(jnp.bfloat16)
+
+    def place(hit):
+        return jnp.dot(jnp.where(hit, 1.0, 0.0).astype(jnp.bfloat16), tri, preferred_element_type=jnp.float32)
+
+    def table(rows, columns):
+        lane = shape_iota(rows, 1)
+        held = jnp.zeros((rows, LANE), jnp.float32)
+        for n, (mask, value) in enumerate(columns):
+            held = jnp.where(lane == n, jnp.sum(jnp.where(mask, value, 0.0), axis=1, keepdims=True), held)
+        return held.astype(jnp.int32)
+
+    to_map = block_map[pl.ds(k_to * 16, 16), :]
+    hit = (to_map >> 6) == g
+    rank = place(hit)
+    half = shape_iota(16, 1) >> 6
+    value = (to_map & 63).astype(jnp.float32)
+    send_tab[...] = table(16, [(hit & (rank == r + 1.0) & (half == h), value) for h in range(2) for r in range(CAP)])
+
+    at = pl.ds(k * 16 + div(g, 2), 1)
+    mine = block_map[at, :]
+    ids = shape_iota(1, 1) & 63
+    left_lim = counts[k, 0] - (g * 64 + ids) * BLK
+    right_lim = counts[k_from, 0] - mine * BLK
+    hit = (shape_iota(NS, 0) == (mine >> 6)) & ((shape_iota(NS, 1) >> 6) == rem(g, 2))
+    rank = place(hit)
+    recv_tab[...] = table(NS, [(hit & (rank == r + 1.0), v.astype(jnp.float32))
+                               for v in (ids, wrap[at, :], left_lim, right_lim) for r in range(CAP)])
+    for copy in copies:
+        copy.wait()
+
+
+def kernel(send_tab, recv_tab, cin, out, send, recv, relay, left, acc, rs1, rs2, rs3,
+           ssem, rsem, lsem, fsem, s1sem, r1sem, s2sem, r2sem, s3sem, r3sem):
     k = lax.axis_index("ka")
     g = lax.axis_index("ga")
     x, z, c = div(g, 16), rem(div(g, 2), NZ), rem(g, 2)
@@ -58,11 +106,37 @@
 
     barrier = pltpu.get_barrier_semaphore()
 
-    def greet(s, carry):
-        pl.semaphore_signal(barrier, inc=1, device_id=(k_from, s), device_id_type=MESH)
-        return carry
-
-    lax.fori_loop(0, NS, greet, 0)
+    even = rem(k, 2) == 0
+    k_relay = rem(k + 6, 8)
+    flipped = (1 - x) * 16 + z * 2 + c
+
+    def greet(kk, steps):
+        def one(grp, carry):
+            for u in steps:
+                s = shifted(x, z, c, offset(grp, u), -1)
+                pl.semaphore_signal(barrier, inc=1, device_id=(kk, s), device_id_type=MESH)
+            return carry
+
+        lax.fori_loop(0, NG, one, 0)
+
+    greet(k_from, DIRECT)
+
+    @pl.when(even)
+    def _():
+        greet(k_from, RELAYED)
+
+        def one(grp, carry):
+            for u in RELAYED:
+                s = x * 16 + rem(shifted(x, z, c, offset(grp, u), -1), 16)
+                pl.semaphore_signal(barrier, inc=1, device_id=(rem(k + 2, 8), s), device_id_type=MESH)
+            return carry
+
+        lax.fori_loop(0, NG, one, 0)
+
+    @pl.when(rem(k, 2) == 1)
+    def _():
+        pl.semaphore_signal(barrier, inc=1, device_id=(k_to, flipped), device_id_type=MESH)
+
     for peer in [core_peer, x_peer] + [z_peer(dz) for dz in range(1, NZ)]:
         pl.semaphore_signal(barrier, inc=1, device_id=(k, peer), device_id_type=MESH)
 
@@ -71,7 +145,7 @@
         for u in range(GRP):
             t = shifted(x, z, c, offset(grp, u), 1)
             for r in range(CAP):
-                send[q, grp * GRP + u, r * ROWS:(r + 1) * ROWS, :] = cin[q, send_tab[t * CAP + r]]
+                send[q, grp * GRP + u, r * ROWS:(r + 1) * ROWS, :] = cin[q, send_tab[div(t, 2), rem(t, 2) * CAP + r]]
 
     def exchange(it, u):
         q, grp = div(it, NG), rem(it, NG)
@@ -81,9 +155,42 @@
             src_ref=send.at[q, j], dst_ref=recv.at[q, j], send_sem=ssem.at[q, j], recv_sem=rsem.at[q, j],
             device_id=(k_to, t), device_id_type=MESH)
 
+    def to_relay(it, n):
+        q, grp = div(it, NG), rem(it, NG)
+        t = x * 16 + rem(shifted(x, z, c, offset(grp, RELAYED[n]), 1), 16)
+        return pltpu.make_async_remote_copy(
+            src_ref=send.at[q, grp * GRP + RELAYED[n]], dst_ref=relay.at[q, grp * NR + n],
+            send_sem=ssem.at[q, grp * GRP + RELAYED[n]], recv_sem=lsem.at[q, grp * NR + n],
+            device_id=(k_relay, t), device_id_type=MESH)
+
+    def forward(it, n):
+        q, grp = div(it, NG), rem(it, NG)
+        j = grp * GRP + RELAYED[n]
+        return pltpu.make_async_remote_copy(
+            src_ref=relay.at[q, grp * NR + n], dst_ref=recv.at[q, j],
+            send_sem=fsem.at[q, grp * NR + n], recv_sem=rsem.at[q, j],
+            device_id=(k_from, flipped), device_id_type=MESH)
+
     def launch(it):
-        for u in range(GRP):
+        @pl.when(even)
+        def _():
+            for n in range(NR):
+                to_relay(it, n).start()
+
+        @pl.when(rem(k, 2) == 1)
+        def _():
+            for u in RELAYED:
+                exchange(it, u).start()
+
+        for u in DIRECT:
             exchange(it, u).start()
+
+    def pass_on(it):
+        @pl.when(even)
+        def _():
+            for n in range(NR):
+                to_relay(it, n).wait_recv()
+                forward(it, n).start()
 
     row = lax.broadcasted_iota(jnp.int32, (2 * ROWS, 4 * ROWS), 0)
     col = lax.broadcasted_iota(jnp.int32, (2 * ROWS, 4 * ROWS), 1)
@@ -103,7 +210,7 @@
             for h in range(2):
                 u, r = divmod(2 * pair + h, CAP)
                 s = shifted(x, z, c, offset(grp, u), -1)
-                slots.append([recv_tab[n * NS * CAP + s * CAP + r] for n in range(4)])
+                slots.append([recv_tab[s, n * CAP + r] for n in range(4)])
             (b0, w0, l0, r0), (b1, w1, l1, r1) = slots
             w = jnp.where(first, w0, w1)
             hit = left_lane == ((right_lane - w) & (BLK - 1))
@@ -192,7 +299,7 @@
         out[1, :, q * LANE:(q + 1) * LANE] = total[16:]
 
     stage(jnp.int32(0))
-    pl.semaphore_wait(barrier, NS + 2 + NZ - 1)
+    pl.semaphore_wait(barrier, NS + 2 + NZ - 1 + (1 - rem(k, 2)))
 
     def start(it, carry):
         launch(it)
@@ -229,6 +336,7 @@
         def _():
             after_x(q - 1)
 
+        pass_on(it)
         multiply(it)
         return carry
 
@@ -243,6 +351,12 @@
     def drain(it, carry):
         for u in range(GRP):
             exchange(it, u).wait_send()
+
+        @pl.when(even)
+        def _():
+            for n in range(NR):
+                forward(it, n).wait_send()
+
         return carry
 
     lax.fori_loop(0, total_its, drain, 0)
@@ -253,31 +367,24 @@
             to_z(q, dz).wait_send()
 
 
-def slots(hit, values):
-    depth = hit.shape[-1]
-    tri = (jnp.arange(depth)[:, None] <= jnp.arange(depth)[None, :]).astype(jnp.bfloat16)
-    place = jnp.dot(hit.astype(jnp.bfloat16), tri, preferred_element_type=jnp.float32).astype(jnp.int32) - 1
-    chosen = hit[:, None, :] & (place[:, None, :] == jnp.arange(CAP)[None, :, None])
-    return [jnp.sum(jnp.where(chosen, v, 0), axis=-1).reshape(-1) for v in values]
-
-
 def local(coeffs, counts, block_map, wrap):
-    k = lax.axis_index("ka")
-    g = lax.axis_index("ga")
-    per = block_map.shape[-1] // NS
-    shard = jnp.arange(NS, dtype=jnp.int32)
-    to_map = block_map[(k + 7) % 8, 0].reshape(NS, per)
-    (send_tab,) = slots(to_map // per == g, [to_map[:, None, :] % per])
-    mine = lax.dynamic_slice_in_dim(block_map[k, 0], g * per, per)
-    turn = lax.dynamic_slice_in_dim(wrap[k, 0], g * per, per)
-    ids = jnp.arange(per, dtype=jnp.int32)
-    left_lim = counts[k, 0] - (g * per + ids) * BLK
-    right_lim = counts[(k + 1) % 8, 0] - mine * BLK
-    recv_tab = jnp.concatenate(slots(mine[None, :] // per == shard[:, None], [ids, turn, left_lim, right_lim]))
-    cin = coeffs.reshape(per, BLK, 2, NQ, LANE).transpose(3, 0, 1, 2, 4).reshape(NQ, per, ROWS, LANE)
+    _, _, rows, parts, bands = coeffs.shape
     vmem = pl.BlockSpec(memory_space=pltpu.VMEM)
     smem = pl.BlockSpec(memory_space=pltpu.SMEM)
     dma = pltpu.SemaphoreType.DMA
+    cin, send_tab, recv_tab = pl.pallas_call(
+        prepare,
+        out_shape=[
+            jax.ShapeDtypeStruct((NQ, rows, parts, LANE), coeffs.dtype),
+            jax.ShapeDtypeStruct((16, LANE), jnp.int32),
+            jax.ShapeDtypeStruct((NS, LANE), jnp.int32),
+        ],
+        in_specs=[smem, vmem, vmem, pl.BlockSpec(memory_space=pltpu.HBM)],
+        out_specs=[vmem, vmem, vmem],
+        scratch_shapes=[dma((NQ,))],
+        compiler_params=pltpu.CompilerParams(vmem_limit_bytes=8 << 20),
+    )(counts, block_map.reshape(-1, LANE), wrap.reshape(-1, LANE), coeffs.reshape(rows, parts, bands))
+    cin = cin.reshape(NQ, rows // BLK, ROWS, LANE)
     out = pl.pallas_call(
         kernel,
         out_shape=jax.ShapeDtypeStruct((2, 16, NQ * LANE), jnp.float32),
@@ -286,12 +393,14 @@
         scratch_shapes=[
             pltpu.VMEM((NQ, NS, STEP, LANE), jnp.bfloat16),
             pltpu.VMEM((NQ, NS, STEP, LANE), jnp.bfloat16),
+            pltpu.VMEM((NQ, NG * NR, STEP, LANE), jnp.bfloat16),
             pltpu.VMEM((1024, NS * STEP), jnp.bfloat16),
             pltpu.VMEM((NQ, 1024, LANE), jnp.float32),
             pltpu.VMEM((NQ, 512, LANE), jnp.float32),
             pltpu.VMEM((NQ, 256, LANE), jnp.float32),
             pltpu.VMEM((NQ, NZ, 32, LANE), jnp.float32),
-            dma((NQ, NS)), dma((NQ, NS)), dma((NQ,)), dma((NQ,)), dma((NQ,)), dma((NQ,)),
+            dma((NQ, NS)), dma((NQ, NS)), dma((NQ, NG * NR)), dma((NQ, NG * NR)),
+            dma((NQ,)), dma((NQ,)), dma((NQ,)), dma((NQ,)),
             dma((NQ, NZ)), dma((NQ, NZ)),
         ],
         compiler_params=pltpu.CompilerParams(

time: 230 us -> 194 us (0.84); the launches traced: 226 us -> 194 us
  local copies, waits for them, and re-layouts: 22.7 us -> 5.28 us
  Pallas kernels: 200 us -> 188 us
  other arithmetic: 2.67 us -> 0 us
    reshape x7 -> x0, local copies, waits for them, and re-layouts: 17.1 us -> none  [the longest x2 16.6 us: local(): coeffs.reshape(per, BLK, 2, NQ, LANE).transpose(3, 0, 1, 2, 4)]
    pallas_call x1, Pallas kernels: 200 us -> 185 us  [local(): pl.pallas_call(kernel, out_shape=jax.ShapeDtypeStruct((2, 16, NQ * LANE),...]
    pallas_call x0 -> x1, Pallas kernels: none -> 3.79 us  [local(): pl.pallas_call(prepare, out_shape=[jax.ShapeDtypeStruct((NQ, rows, parts,...]
    unnamed x4 -> x7, local copies, waits for them, and re-layouts: 2.19 us -> 4.59 us
where the time goes in v2:
time: 194 us
  Pallas kernels  188 us (97%)
  local copies, waits for them, and re-layouts  5.28 us (3%)
    pallas_call x1, Pallas kernels, local(): pl.pallas_call(kernel, out_shape=jax.ShapeDtypeStruct((2, 16, NQ * LANE),...  185 us
    unnamed x7, local copies, waits for them, and re-layouts  4.59 us

profile of v2, /device:TPU:10, one launch (start us, length us, event | category | flops | bytes accessed | tf_op | source)
XLA Modules:
  0.0 193.7 jit_solution(15887294097790906371)
XLA Ops:
  0.0 0.7 copy.5.counts
  0.7 0.0 copy-start
  0.7 2.2 %copy-done = bf16[1,1,2048,2,512]{4,3,2,1,0:T(2,128)(2,1)S(1)} copy-done((bf16[1,1,2048,2,512]{4,3,2,1,0:T(2,128)(2,1)S(1)}, bf16[1,1,2048,2,512]{4,3,2,1,0:T(2,128)(2,1)}, u32[]{:S(2)}) %copy-start) | copy-done | bytes 4194328
  2.9 0.0 copy-start.1
  2.9 0.8 copy-done.1
  3.8 0.0 copy-start.2
  3.8 0.8 copy-done.2
  4.6 3.8 %shard_map.46 = (bf16[4,2048,2,128]{3,2,1,0:T(2,128)(2,1)S(1)}, s32[16,128]{1,0:T(8,128)S(1)}, s32[32,128]{1,0:T(8,128)S(1)}) custom-call(s32[8,1]{1,0:T(8,128)S(1)} %copy.5.counts, s32[128,128]{1,0:T(8,128)S(1)} %bitcast.10, s32[128,128]{1,0:T(8,128)S(1)} %bitcast.11, bf16[2048,2,512]{2,1,0:T(2,128)(2,1)S(1)} %bitcast.7), custom_call_target="tpu_custom_call" | custom-call | tf_op jit(solution)/shard_map/pallas_call | solution.py:375
  8.4 184.6 %shard_map.47 = f32[2,16,512]{2,1,0:T(8,128)S(1)} custom-call(s32[16,128]{1,0:T(8,128)S(1)} %get-tuple-element.8.send_tab, s32[32,128]{1,0:T(8,128)S(1)} %get-tuple-element.9.recv_tab, bf16[4,64,64,128]{3,2,1,0:T(8,128)(2,1)S(1)} %bitcast.8), custom_call_target="tpu_custom_call" | custom-call | tf_op jit(solution)/shard_map/pallas_call | solution.py:388
  193.0 0.7 copy.6
Async XLA Ops:
  0.7 2.2 %copy-start = (bf16[1,1,2048,2,512]{4,3,2,1,0:T(2,128)(2,1)S(1)}, bf16[1,1,2048,2,512]{4,3,2,1,0:T(2,128)(2,1)}, u32[]{:S(2)}) copy-start(bf16[1,1,2048,2,512]{4,3,2,1,0:T(2,128)(2,1)} %param.4) | copy-start | bytes 12582916
  2.9 0.8 copy-start.1
  3.8 0.8 copy-start.2

commit v3 on v2

--- a/solution.py
+++ b/solution.py
@@ -13,15 +13,18 @@
 CAP = 3
 NS = 32
 NZ = 8
+NX = 2
 LANE = 128
 NQ = 4
 GRP = 4
 NG = NS // GRP
 STEP = CAP * ROWS
-AHEAD = 4
+AHEAD = 20
 RELAYED = (1, 2)
 DIRECT = (0, 3)
 NR = len(RELAYED)
+TOTAL = NQ * NG
+RELAY_END = TOTAL - 3
 
 
 def rem(a, b):
@@ -48,52 +51,46 @@
     return rem(x + dx, 2) * 16 + rem(z + sign * dz + 16, NZ) * 2 + rem(c + dc, 2)
 
 
-def prepare(counts, block_map, wrap, coeffs, cin, send_tab, recv_tab, sem):
-    copies = [pltpu.make_async_copy(coeffs.at[:, :, pl.ds(q * LANE, LANE)], cin.at[q], sem.at[q]) for q in range(NQ)]
-    for copy in copies:
-        copy.start()
-    k = lax.axis_index("ka")
-    g = lax.axis_index("ga")
-    k_to, k_from = rem(k + 7, 8), rem(k + 1, 8)
-
-    def shape_iota(rows, dim):
-        return lax.broadcasted_iota(jnp.int32, (rows, LANE), dim)
-
-    tri = (shape_iota(LANE, 0) <= shape_iota(LANE, 1)) & (div(shape_iota(LANE, 0), 64) == div(shape_iota(LANE, 1), 64))
-    tri = jnp.where(tri, 1.0, 0.0).astype(jnp.bfloat16)
-
+def iota(rows, dim):
+    return lax.broadcasted_iota(jnp.int32, (rows, LANE), dim)
+
+
+def make_tables(k, g, counts, maps, send_tab, recv_tab):
     def place(hit):
-        return jnp.dot(jnp.where(hit, 1.0, 0.0).astype(jnp.bfloat16), tri, preferred_element_type=jnp.float32)
+        lane = iota(hit.shape[0], 1) & 63
+        count = jnp.where(hit, 1, 0)
+        for shift in (1, 2, 4, 8, 16, 32):
+            count = count + jnp.where(lane >= shift, pltpu.roll(count, shift, 1), 0)
+        return count
 
     def table(rows, columns):
-        lane = shape_iota(rows, 1)
-        held = jnp.zeros((rows, LANE), jnp.float32)
+        lane = iota(rows, 1)
+        held = jnp.zeros((rows, LANE), jnp.int32)
         for n, (mask, value) in enumerate(columns):
-            held = jnp.where(lane == n, jnp.sum(jnp.where(mask, value, 0.0), axis=1, keepdims=True), held)
-        return held.astype(jnp.int32)
-
-    to_map = block_map[pl.ds(k_to * 16, 16), :]
+            held = jnp.where(lane == n, jnp.sum(jnp.where(mask, value, 0), axis=1, keepdims=True), held)
+        return held
+
+    to_map = maps[0]
     hit = (to_map >> 6) == g
     rank = place(hit)
-    half = shape_iota(16, 1) >> 6
-    value = (to_map & 63).astype(jnp.float32)
-    send_tab[...] = table(16, [(hit & (rank == r + 1.0) & (half == h), value) for h in range(2) for r in range(CAP)])
-
-    at = pl.ds(k * 16 + div(g, 2), 1)
-    mine = block_map[at, :]
-    ids = shape_iota(1, 1) & 63
-    left_lim = counts[k, 0] - (g * 64 + ids) * BLK
-    right_lim = counts[k_from, 0] - mine * BLK
-    hit = (shape_iota(NS, 0) == (mine >> 6)) & ((shape_iota(NS, 1) >> 6) == rem(g, 2))
+    half = iota(16, 1) >> 6
+    value = to_map & 63
+    send_tab[...] = table(16, [(hit & (rank == r + 1) & (half == h), value) for h in range(2) for r in range(CAP)])
+
+    at = pl.ds(div(g, 2), 1)
+    mine = maps[1, at, :]
+    ids = iota(1, 1) & 63
+    left_lim = counts[k] - (g * 64 + ids) * BLK
+    right_lim = counts[rem(k + 1, 8)] - mine * BLK
+    hit = (iota(NS, 0) == (mine >> 6)) & ((iota(NS, 1) >> 6) == rem(g, 2))
     rank = place(hit)
-    recv_tab[...] = table(NS, [(hit & (rank == r + 1.0), v.astype(jnp.float32))
-                               for v in (ids, wrap[at, :], left_lim, right_lim) for r in range(CAP)])
-    for copy in copies:
-        copy.wait()
-
-
-def kernel(send_tab, recv_tab, cin, out, send, recv, relay, left, acc, rs1, rs2, rs3,
-           ssem, rsem, lsem, fsem, s1sem, r1sem, s2sem, r2sem, s3sem, r3sem):
+    recv_tab[...] = table(NS, [(hit & (rank == r + 1), v)
+                               for v in (ids, maps[2, at, :], left_lim, right_lim) for r in range(CAP)])
+
+
+def kernel(counts, block_map, wrap, coeffs, out, cin, maps, send_vec, recv_vec, send_tab, recv_tab,
+           send, recv, relay, left, flat, acc, rs1, rs2, rs3, rs4, csem, map_sem, tab_sem,
+           ssem, rsem, lsem, fsem, s1sem, r1sem, s2sem, r2sem, s3sem, r3sem, s4sem, r4sem):
     k = lax.axis_index("ka")
     g = lax.axis_index("ga")
     x, z, c = div(g, 16), rem(div(g, 2), NZ), rem(g, 2)
@@ -101,8 +98,17 @@
     core_peer = x * 16 + z * 2 + (1 - c)
     x_peer = (1 - x) * 16 + z * 2 + c
 
-    def z_peer(dz):
-        return x * 16 + rem(z + dz, NZ) * 2 + c
+    def any_peer(dx, dz):
+        return rem(x + dx, NX) * 16 + rem(z + dz, NZ) * 2 + c
+
+    def map_rows(kk):
+        return pl.ds(pl.multiple_of(kk * 16, 16), 16)
+
+    fetches = [pltpu.make_async_copy(source.at[map_rows(kk)], maps.at[n], map_sem.at[n])
+               for n, (source, kk) in enumerate(((block_map, k_to), (block_map, k), (wrap, k)))]
+    copies = [pltpu.make_async_copy(coeffs.at[:, :, pl.ds(q * LANE, LANE)], cin.at[q], csem.at[q]) for q in range(NQ)]
+    for copy in fetches + copies:
+        copy.start()
 
     barrier = pltpu.get_barrier_semaphore()
 
@@ -119,12 +125,10 @@
 
         lax.fori_loop(0, NG, one, 0)
 
-    greet(k_from, DIRECT)
+    greet(k_from, range(GRP))
 
     @pl.when(even)
     def _():
-        greet(k_from, RELAYED)
-
         def one(grp, carry):
             for u in RELAYED:
                 s = x * 16 + rem(shifted(x, z, c, offset(grp, u), -1), 16)
@@ -137,7 +141,7 @@
     def _():
         pl.semaphore_signal(barrier, inc=1, device_id=(k_to, flipped), device_id_type=MESH)
 
-    for peer in [core_peer, x_peer] + [z_peer(dz) for dz in range(1, NZ)]:
+    for peer in [core_peer] + [any_peer(dx, dz) for dx in range(NX) for dz in range(NZ) if dx or dz]:
         pl.semaphore_signal(barrier, inc=1, device_id=(k, peer), device_id_type=MESH)
 
     def stage(it):
@@ -145,7 +149,8 @@
         for u in range(GRP):
             t = shifted(x, z, c, offset(grp, u), 1)
             for r in range(CAP):
-                send[q, grp * GRP + u, r * ROWS:(r + 1) * ROWS, :] = cin[q, send_tab[div(t, 2), rem(t, 2) * CAP + r]]
+                blk = send_tab[div(t, 2), rem(t, 2) * CAP + r] & 63
+                send[q, grp * GRP + u, r * BLK:(r + 1) * BLK] = cin[q, pl.ds(blk * BLK, BLK)]
 
     def exchange(it, u):
         q, grp = div(it, NG), rem(it, NG)
@@ -172,12 +177,12 @@
             device_id=(k_from, flipped), device_id_type=MESH)
 
     def launch(it):
-        @pl.when(even)
+        @pl.when(even & (it < RELAY_END))
         def _():
             for n in range(NR):
                 to_relay(it, n).start()
 
-        @pl.when(rem(k, 2) == 1)
+        @pl.when(jnp.logical_not(even & (it < RELAY_END)))
         def _():
             for u in RELAYED:
                 exchange(it, u).start()
@@ -186,7 +191,7 @@
             exchange(it, u).start()
 
     def pass_on(it):
-        @pl.when(even)
+        @pl.when(even & (it < RELAY_END))
         def _():
             for n in range(NR):
                 to_relay(it, n).wait_recv()
@@ -218,7 +223,7 @@
             pick = jnp.where(hit, pattern, 0.0).astype(jnp.bfloat16)
             cols = pl.ds(pl.multiple_of(grp * (GRP * STEP) + pair * 2 * ROWS, LANE), 2 * ROWS)
             for q in range(NQ):
-                held = jnp.concatenate([cin[q, b0], cin[q, b1]], axis=0)
+                held = jnp.concatenate([cin[q, pl.ds((b & 63) * BLK, BLK)].reshape(ROWS, LANE) for b in (b0, b1)], axis=0)
                 moved = lax.dot_general(held, pick, (((0,), (0,)), ((), ())),
                                         preferred_element_type=jnp.float32).astype(jnp.bfloat16)
                 for ii in range(8):
@@ -235,12 +240,13 @@
             exchange(it, u).wait_recv()
         j0 = grp * GRP
         cols = pl.ds(pl.multiple_of(grp * (GRP * STEP), LANE), GRP * STEP)
-        right = recv[q, pl.ds(j0, GRP)].reshape(GRP * STEP, LANE)
+        for u in range(GRP):
+            flat[u * STEP:(u + 1) * STEP] = recv[q, j0 + u].reshape(STEP, LANE)
         part = 256
 
         def strip(n, carry):
             rows = pl.ds(pl.multiple_of(n * part, part), part)
-            val = jnp.dot(left[rows, cols], right, preferred_element_type=jnp.float32)
+            val = jnp.dot(left[rows, cols], flat[...], preferred_element_type=jnp.float32)
 
             @pl.when(grp == 0)
             def _():
@@ -277,7 +283,14 @@
         return pltpu.make_async_remote_copy(
             src_ref=acc.at[q, piece(c, x, rem(z + dz, NZ))], dst_ref=rs3.at[q, dz],
             send_sem=s3sem.at[q, dz], recv_sem=r3sem.at[q, dz],
-            device_id=(k, z_peer(dz)), device_id_type=MESH)
+            device_id=(k, any_peer(0, dz)), device_id_type=MESH)
+
+    def to_any(q, dx, dz):
+        n = dx * NZ + dz
+        return pltpu.make_async_remote_copy(
+            src_ref=acc.at[q, piece(c, rem(x + dx, NX), rem(z + dz, NZ))], dst_ref=rs4.at[n],
+            send_sem=s4sem.at[n], recv_sem=r4sem.at[n],
+            device_id=(k, any_peer(dx, dz)), device_id_type=MESH)
 
     def after_core(q):
         to_core(q).wait_recv()
@@ -298,8 +311,34 @@
         out[0, :, q * LANE:(q + 1) * LANE] = total[:16]
         out[1, :, q * LANE:(q + 1) * LANE] = total[16:]
 
+    far_first = sorted(((dx, dz) for dx in range(NX) for dz in range(NZ) if dx or dz),
+                       key=lambda p: -min(p[1], NZ - p[1]))
+
+    def spread(q):
+        to_core(q).wait_recv()
+        acc[q, half(c)] += rs1[q]
+        for dx, dz in far_first:
+            to_any(q, dx, dz).start()
+
+    def finish_last(q):
+        total = acc[q, piece(c, x, z)]
+        for dx, dz in reversed(far_first):
+            to_any(q, dx, dz).wait_recv()
+            total = total + rs4[dx * NZ + dz]
+        out[0, :, q * LANE:(q + 1) * LANE] = total[:16]
+        out[1, :, q * LANE:(q + 1) * LANE] = total[16:]
+
+    for copy in fetches:
+        copy.wait()
+    make_tables(k, g, counts, maps, send_vec, recv_vec)
+    tables = [pltpu.make_async_copy(vec, tab, tab_sem.at[n])
+              for n, (vec, tab) in enumerate(((send_vec, send_tab), (recv_vec, recv_tab)))]
+    for copy in tables:
+        copy.start()
+    for copy in tables + copies:
+        copy.wait()
     stage(jnp.int32(0))
-    pl.semaphore_wait(barrier, NS + 2 + NZ - 1 + (1 - rem(k, 2)))
+    pl.semaphore_wait(barrier, NS + NX * NZ + (1 - rem(k, 2)) * 17)
 
     def start(it, carry):
         launch(it)
@@ -307,16 +346,15 @@
         return carry
 
     lax.fori_loop(0, AHEAD, start, 0)
-    total_its = NQ * NG
 
     def body(it, carry):
         q, grp = div(it, NG), rem(it, NG)
 
-        @pl.when(it + AHEAD < total_its)
+        @pl.when(it + AHEAD < TOTAL)
         def _():
             launch(it + AHEAD)
 
-        @pl.when(it + AHEAD + 1 < total_its)
+        @pl.when(it + AHEAD + 1 < TOTAL)
         def _():
             stage(it + AHEAD + 1)
 
@@ -340,72 +378,71 @@
         multiply(it)
         return carry
 
-    lax.fori_loop(0, total_its, body, 0)
+    lax.fori_loop(0, TOTAL, body, 0)
     last = NQ - 1
     to_core(last).start()
-    after_core(last)
-    after_x(last)
-    for q in range(NQ):
+    spread(last)
+    for q in range(last):
         finish(q)
+    finish_last(last)
 
     def drain(it, carry):
         for u in range(GRP):
             exchange(it, u).wait_send()
 
-        @pl.when(even)
+        @pl.when(even & (it < RELAY_END))
         def _():
             for n in range(NR):
                 forward(it, n).wait_send()
 
         return carry
 
-    lax.fori_loop(0, total_its, drain, 0)
+    lax.fori_loop(0, TOTAL, drain, 0)
     for q in range(NQ):
         to_core(q).wait_send()
+    for q in range(last):
         to_x(q).wait_send()
         for dz in range(1, NZ):
             to_z(q, dz).wait_send()
+    for dx, dz in far_first:
+        to_any(last, dx, dz).wait_send()
 
 
 def local(coeffs, counts, block_map, wrap):
     _, _, rows, parts, bands = coeffs.shape
-    vmem = pl.BlockSpec(memory_space=pltpu.VMEM)
     smem = pl.BlockSpec(memory_space=pltpu.SMEM)
+    hbm = pl.BlockSpec(memory_space=pltpu.HBM)
     dma = pltpu.SemaphoreType.DMA
-    cin, send_tab, recv_tab = pl.pallas_call(
-        prepare,
-        out_shape=[
-            jax.ShapeDtypeStruct((NQ, rows, parts, LANE), coeffs.dtype),
-            jax.ShapeDtypeStruct((16, LANE), jnp.int32),
-            jax.ShapeDtypeStruct((NS, LANE), jnp.int32),
-        ],
-        in_specs=[smem, vmem, vmem, pl.BlockSpec(memory_space=pltpu.HBM)],
-        out_specs=[vmem, vmem, vmem],
-        scratch_shapes=[dma((NQ,))],
-        compiler_params=pltpu.CompilerParams(vmem_limit_bytes=8 << 20),
-    )(counts, block_map.reshape(-1, LANE), wrap.reshape(-1, LANE), coeffs.reshape(rows, parts, bands))
-    cin = cin.reshape(NQ, rows // BLK, ROWS, LANE)
     out = pl.pallas_call(
         kernel,
         out_shape=jax.ShapeDtypeStruct((2, 16, NQ * LANE), jnp.float32),
-        in_specs=[smem, smem, vmem],
-        out_specs=vmem,
+        in_specs=[smem, hbm, hbm, hbm],
+        out_specs=pl.BlockSpec(memory_space=pltpu.VMEM),
         scratch_shapes=[
-            pltpu.VMEM((NQ, NS, STEP, LANE), jnp.bfloat16),
-            pltpu.VMEM((NQ, NS, STEP, LANE), jnp.bfloat16),
-            pltpu.VMEM((NQ, NG * NR, STEP, LANE), jnp.bfloat16),
+            pltpu.VMEM((NQ, rows, parts, LANE), coeffs.dtype),
+            pltpu.VMEM((3, 16, LANE), jnp.int32),
+            pltpu.VMEM((16, LANE), jnp.int32),
+            pltpu.VMEM((NS, LANE), jnp.int32),
+            pltpu.SMEM((16, LANE), jnp.int32),
+            pltpu.SMEM((NS, LANE), jnp.int32),
+            pltpu.VMEM((NQ, NS, STEP // 2, 2, LANE), jnp.bfloat16),
+            pltpu.VMEM((NQ, NS, STEP // 2, 2, LANE), jnp.bfloat16),
+            pltpu.VMEM((NQ, NG * NR, STEP // 2, 2, LANE), jnp.bfloat16),
             pltpu.VMEM((1024, NS * STEP), jnp.bfloat16),
+            pltpu.VMEM((GRP * STEP, LANE), jnp.bfloat16),
             pltpu.VMEM((NQ, 1024, LANE), jnp.float32),
             pltpu.VMEM((NQ, 512, LANE), jnp.float32),
             pltpu.VMEM((NQ, 256, LANE), jnp.float32),
-            pltpu.VMEM((NQ, NZ, 32, LANE), jnp.float32),
+            pltpu.VMEM((NQ - 1, NZ, 32, LANE), jnp.float32),
+            pltpu.VMEM((NX * NZ, 32, LANE), jnp.float32),
+            dma((NQ,)), dma((3,)), dma((2,)),
             dma((NQ, NS)), dma((NQ, NS)), dma((NQ, NG * NR)), dma((NQ, NG * NR)),
             dma((NQ,)), dma((NQ,)), dma((NQ,)), dma((NQ,)),
-            dma((NQ, NZ)), dma((NQ, NZ)),
+            dma((NQ, NZ)), dma((NQ, NZ)), dma((NX * NZ,)), dma((NX * NZ,)),
         ],
         compiler_params=pltpu.CompilerParams(
-            collective_id=0, has_side_effects=True, vmem_limit_bytes=48 << 20),
-    )(send_tab, recv_tab, cin)
+            collective_id=0, has_side_effects=True, vmem_limit_bytes=58 << 20),
+    )(counts.reshape(-1), block_map.reshape(-1, LANE), wrap.reshape(-1, LANE), coeffs.reshape(rows, parts, bands))
     return out.transpose(1, 0, 2)[None, :, None]
 
 

time: 194 us -> 173 us (0.89)
  Pallas kernels: 188 us -> 171 us
  local copies, waits for them, and re-layouts: 5.28 us -> 1.52 us
    pallas_call x1, Pallas kernels: 185 us -> 171 us  [local(): pl.pallas_call(kernel, out_shape=jax.ShapeDtypeStruct((2, 16, NQ * LANE),...]
    unnamed x7 -> x0, local copies, waits for them, and re-layouts: 4.59 us -> none
    pallas_call x1 -> x0, Pallas kernels: 3.79 us -> none  [local(): pl.pallas_call(prepare, out_shape=[jax.ShapeDtypeStruct((NQ, rows, parts,...]
where the time goes in v3:
time: 173 us; the launch traced here: 172 us
  Pallas kernels  171 us (99%)
    pallas_call x1, Pallas kernels, local(): pl.pallas_call(kernel, out_shape=jax.ShapeDtypeStruct((2, 16, NQ * LANE),...  171 us

profile of v3, /device:TPU:10, one launch (start us, length us, event | category | flops | bytes accessed | tf_op | source)
XLA Modules:
  0.0 172.5 jit_solution(11676496475046165090)
XLA Ops:
  0.0 171.0 %shard_map.46 = f32[2,16,512]{2,1,0:T(8,128)} custom-call(s32[8]{0:T(128)} %bitcast.11, s32[128,128]{1,0:T(8,128)} %bitcast.9, s32[128,128]{1,0:T(8,128)} %bitcast.10, bf16[2048,2,512]{2,1,0:T(2,128)(2,1)} %bitcast.7), custom_call_target="tpu_custom_call" | custom-call | tf_op jit(solution)/shard_map/pallas_call | solution.py:416
  171.0 1.5 copy.5

commit v4 on v3

--- a/solution.py
+++ b/solution.py
@@ -36,7 +36,7 @@
 
 
 def offset(grp, u):
-    grp = NG - 1 - grp
+    grp = rem(NG - grp, NG)
     d = div(grp + 1, 2)
     edge = 1 - div(rem(grp, 7) + 6, 7)
     odd = u % 2
@@ -244,8 +244,8 @@
             flat[u * STEP:(u + 1) * STEP] = recv[q, j0 + u].reshape(STEP, LANE)
         part = 256
 
-        def strip(n, carry):
-            rows = pl.ds(pl.multiple_of(n * part, part), part)
+        def strip(owner, n):
+            rows = pl.ds(pl.multiple_of(owner * 512 + n * part, part), part)
             val = jnp.dot(left[rows, cols], flat[...], preferred_element_type=jnp.float32)
 
             @pl.when(grp == 0)
@@ -256,9 +256,15 @@
             def _():
                 acc[q, rows] += val
 
-            return carry
-
-        lax.fori_loop(0, 1024 // part, strip, 0)
+        for n in range(2):
+            strip(1 - c, n)
+
+        @pl.when(grp == NG - 1)
+        def _():
+            to_core(q).start()
+
+        for n in range(2):
+            strip(c, n)
 
     def half(which):
         return pl.ds(pl.multiple_of(which * 512, 512), 512)
@@ -362,10 +368,6 @@
         def _():
             build(grp)
 
-        @pl.when((q > 0) & (grp == 0))
-        def _():
-            to_core(q - 1).start()
-
         @pl.when((q > 0) & (grp == 2))
         def _():
             after_core(q - 1)
@@ -380,7 +382,6 @@
 
     lax.fori_loop(0, TOTAL, body, 0)
     last = NQ - 1
-    to_core(last).start()
     spread(last)
     for q in range(last):
         finish(q)

time: 173 us -> 173 us (level)
  no operation moved by 1% of the time
where the time goes in v4:
time: 173 us; the launch traced here: 171 us
  Pallas kernels  170 us (98%)
    pallas_call x1, Pallas kernels, local(): pl.pallas_call(kernel, out_shape=jax.ShapeDtypeStruct((2, 16, NQ * LANE),...  170 us

profile of v4, /device:TPU:10, one launch (start us, length us, event | category | flops | bytes accessed | tf_op | source)
XLA Modules:
  0.0 171.2 jit_solution(5268364364259742776)
XLA Ops:
  0.0 169.6 %shard_map.46 = f32[2,16,512]{2,1,0:T(8,128)} custom-call(s32[8]{0:T(128)} %bitcast.11, s32[128,128]{1,0:T(8,128)} %bitcast.9, s32[128,128]{1,0:T(8,128)} %bitcast.10, bf16[2048,2,512]{2,1,0:T(2,128)(2,1)} %bitcast.7), custom_call_target="tpu_custom_call" | custom-call | tf_op jit(solution)/shard_map/pallas_call | solution.py:417
  169.6 1.5 copy.5

commit v5 on v4

--- a/solution.py
+++ b/solution.py
@@ -19,12 +19,12 @@
 GRP = 4
 NG = NS // GRP
 STEP = CAP * ROWS
-AHEAD = 20
+AHEAD = 23
 RELAYED = (1, 2)
 DIRECT = (0, 3)
 NR = len(RELAYED)
 TOTAL = NQ * NG
-RELAY_END = TOTAL - 3
+RELAY_END = TOTAL - 2
 
 
 def rem(a, b):
@@ -88,7 +88,7 @@
                                for v in (ids, maps[2, at, :], left_lim, right_lim) for r in range(CAP)])
 
 
-def kernel(counts, block_map, wrap, coeffs, out, cin, maps, send_vec, recv_vec, send_tab, recv_tab,
+def kernel(counts, block_map, wrap, coeffs, out, cin, cin0, maps, send_vec, recv_vec, send_tab, recv_tab,
            send, recv, relay, left, flat, acc, rs1, rs2, rs3, rs4, csem, map_sem, tab_sem,
            ssem, rsem, lsem, fsem, s1sem, r1sem, s2sem, r2sem, s3sem, r3sem, s4sem, r4sem):
     k = lax.axis_index("ka")
@@ -106,7 +106,8 @@
 
     fetches = [pltpu.make_async_copy(source.at[map_rows(kk)], maps.at[n], map_sem.at[n])
                for n, (source, kk) in enumerate(((block_map, k_to), (block_map, k), (wrap, k)))]
-    copies = [pltpu.make_async_copy(coeffs.at[:, :, pl.ds(q * LANE, LANE)], cin.at[q], csem.at[q]) for q in range(NQ)]
+    copies = [pltpu.make_async_copy(coeffs.at[:, :, pl.ds(q * LANE, LANE)], dst, csem.at[n])
+              for n, (q, dst) in enumerate([(0, cin0)] + [(q, cin.at[q]) for q in range(NQ)])]
     for copy in fetches + copies:
         copy.start()
 
@@ -144,13 +145,14 @@
     for peer in [core_peer] + [any_peer(dx, dz) for dx in range(NX) for dz in range(NZ) if dx or dz]:
         pl.semaphore_signal(barrier, inc=1, device_id=(k, peer), device_id_type=MESH)
 
-    def stage(it):
+    def stage(it, held=None):
         q, grp = div(it, NG), rem(it, NG)
         for u in range(GRP):
             t = shifted(x, z, c, offset(grp, u), 1)
             for r in range(CAP):
                 blk = send_tab[div(t, 2), rem(t, 2) * CAP + r] & 63
-                send[q, grp * GRP + u, r * BLK:(r + 1) * BLK] = cin[q, pl.ds(blk * BLK, BLK)]
+                rows = pl.ds(blk * BLK, BLK)
+                send[q, grp * GRP + u, r * BLK:(r + 1) * BLK] = cin[q, rows] if held is None else held[rows]
 
     def exchange(it, u):
         q, grp = div(it, NG), rem(it, NG)
@@ -175,6 +177,11 @@
             src_ref=relay.at[q, grp * NR + n], dst_ref=recv.at[q, j],
             send_sem=fsem.at[q, grp * NR + n], recv_sem=rsem.at[q, j],
             device_id=(k_from, flipped), device_id_type=MESH)
+
+    def arrival(q, j):
+        return pltpu.make_async_remote_copy(
+            src_ref=send.at[q, j], dst_ref=recv.at[q, j], send_sem=ssem.at[q, j], recv_sem=rsem.at[q, j],
+            device_id=(k_to, g), device_id_type=MESH)
 
     def launch(it):
         @pl.when(even & (it < RELAY_END))
@@ -236,35 +243,37 @@
 
     def multiply(it):
         q, grp = div(it, NG), rem(it, NG)
+        cols = pl.ds(pl.multiple_of(grp * (GRP * STEP), LANE), GRP * STEP)
+        part = 256
         for u in range(GRP):
-            exchange(it, u).wait_recv()
-        j0 = grp * GRP
-        cols = pl.ds(pl.multiple_of(grp * (GRP * STEP), LANE), GRP * STEP)
-        for u in range(GRP):
-            flat[u * STEP:(u + 1) * STEP] = recv[q, j0 + u].reshape(STEP, LANE)
-        part = 256
-
-        def strip(owner, n):
-            rows = pl.ds(pl.multiple_of(owner * 512 + n * part, part), part)
-            val = jnp.dot(left[rows, cols], flat[...], preferred_element_type=jnp.float32)
-
-            @pl.when(grp == 0)
-            def _():
-                acc[q, rows] = val
-
-            @pl.when(grp > 0)
-            def _():
-                acc[q, rows] += val
-
-        for n in range(2):
-            strip(1 - c, n)
+            j = grp * GRP + u
+            arrival(q, j).wait_recv()
+            flat[u * STEP:(u + 1) * STEP] = recv[q, j].reshape(STEP, LANE)
+
+        def strips(owner):
+            def strip(n, carry):
+                rows = pl.ds(pl.multiple_of(owner * 512 + n * part, part), part)
+                val = jnp.dot(left[rows, cols], flat[...], preferred_element_type=jnp.float32)
+
+                @pl.when(grp == 0)
+                def _():
+                    acc[q, rows] = val
+
+                @pl.when(grp > 0)
+                def _():
+                    acc[q, rows] += val
+
+                return carry
+
+            lax.fori_loop(0, 512 // part, strip, 0)
+
+        strips(1 - c)
 
         @pl.when(grp == NG - 1)
         def _():
             to_core(q).start()
 
-        for n in range(2):
-            strip(c, n)
+        strips(c)
 
     def half(which):
         return pl.ds(pl.multiple_of(which * 512, 512), 512)
@@ -341,17 +350,20 @@
               for n, (vec, tab) in enumerate(((send_vec, send_tab), (recv_vec, recv_tab)))]
     for copy in tables:
         copy.start()
-    for copy in tables + copies:
+    for copy in tables + copies[:1]:
         copy.wait()
-    stage(jnp.int32(0))
+    stage(jnp.int32(0), cin0)
     pl.semaphore_wait(barrier, NS + NX * NZ + (1 - rem(k, 2)) * 17)
 
-    def start(it, carry):
+    def start(it, carry, held=None):
         launch(it)
-        stage(it + 1)
+        stage(it + 1, held)
         return carry
 
-    lax.fori_loop(0, AHEAD, start, 0)
+    lax.fori_loop(0, NG - 1, functools.partial(start, held=cin0), 0)
+    for copy in copies[1:]:
+        copy.wait()
+    lax.fori_loop(NG - 1, AHEAD, start, 0)
 
     def body(it, carry):
         q, grp = div(it, NG), rem(it, NG)
@@ -421,6 +433,7 @@
         out_specs=pl.BlockSpec(memory_space=pltpu.VMEM),
         scratch_shapes=[
             pltpu.VMEM((NQ, rows, parts, LANE), coeffs.dtype),
+            pltpu.VMEM((rows, parts, LANE), coeffs.dtype),
             pltpu.VMEM((3, 16, LANE), jnp.int32),
             pltpu.VMEM((16, LANE), jnp.int32),
             pltpu.VMEM((NS, LANE), jnp.int32),
@@ -436,7 +449,7 @@
             pltpu.VMEM((NQ, 256, LANE), jnp.float32),
             pltpu.VMEM((NQ - 1, NZ, 32, LANE), jnp.float32),
             pltpu.VMEM((NX * NZ, 32, LANE), jnp.float32),
-            dma((NQ,)), dma((3,)), dma((2,)),
+            dma((NQ + 1,)), dma((3,)), dma((2,)),
             dma((NQ, NS)), dma((NQ, NS)), dma((NQ, NG * NR)), dma((NQ, NG * NR)),
             dma((NQ,)), dma((NQ,)), dma((NQ,)), dma((NQ,)),
             dma((NQ, NZ)), dma((NQ, NZ)), dma((NX * NZ,)), dma((NX * NZ,)),

time: 173 us -> 173 us (level)
  no operation moved by 1% of the time
where the time goes in v5:
time: 173 us; the launch traced here: 171 us
  Pallas kernels  169 us (98%)
    pallas_call x1, Pallas kernels, local(): pl.pallas_call(kernel, out_shape=jax.ShapeDtypeStruct((2, 16, NQ * LANE),...  169 us

profile of v5, /device:TPU:10, one launch (start us, length us, event | category | flops | bytes accessed | tf_op | source)
XLA Modules:
  0.0 170.8 jit_solution(1240178127813954570)
XLA Ops:
  0.0 169.3 %shard_map.46 = f32[2,16,512]{2,1,0:T(8,128)} custom-call(s32[8]{0:T(128)} %bitcast.11, s32[128,128]{1,0:T(8,128)} %bitcast.9, s32[128,128]{1,0:T(8,128)} %bitcast.10, bf16[2048,2,512]{2,1,0:T(2,128)(2,1)} %bitcast.7), custom_call_target="tpu_custom_call" | custom-call | tf_op jit(solution)/shard_map/pallas_call | solution.py:429
  169.3 1.5 copy.5
